TPU v7x, 128 devices: a whole 4x4x4 slice. The times are simulated.
128 devices in a mesh: band: 64 (over y, z_lo, x, core), ga: 2 (over z_hi).
Axes of the slice: x: 4, y: 4, z: 4 (z_hi: 2, z_lo: 2; z = z_hi * 2 + z_lo), core: 2. Of those that a mesh axis runs over, the one named last changes fastest.
Arguments:
- matrix_elements: float32 [2, 16384, 12288], P(None, 'band', 'ga'), may hold values from -16 to 16
- band_index: int32 [16384], P('band'), may hold values from 0 to 1048575
- occupied: int32 [1], replicated, may hold values from 262144 to 786432
- band_weight: float32 [16384], P('band'), may hold values from 0.3 to 3
- coulomb: float32 [12288], replicated, may hold values from 0.2 to 5
Outputs:
- sigma: float32 [12288, 2, 512], P(('ga', 'band'))
All inputs are finite; a program needn't handle non-finite values.
Results may differ from a plain program's by a relative error of at most 0.00018.
Values sent between devices are 32-bit elements; how exact they have to be, the bound alone decides.
A program may use at most 192 MiB of HBM per device.

v0:
```python
import math

import jax
import jax.numpy as jnp
from jax import lax
from jax.sharding import Mesh
from jax.sharding import PartitionSpec as P

COLS = 512
BAND = ("band_0", "band_1", "band_2", "band_3")
GA_BAND = ("ga", "band_0", "band_1", "band_2", "band_3")


def spread(x, axis, root):
    mine = lax.axis_index(axis) == root
    return lax.psum(jnp.where(mine, x, jnp.zeros_like(x)), axis)


def in_blocks(x, dim, length):
    before, after = (x.shape[:dim], x.shape[dim + 1 :])
    return jnp.moveaxis(x.reshape(*before, length, -1, *after), dim, 0)


def sum_by_chip(x, chips, core, dim):
    sizes = (lax.axis_size(chips), lax.axis_size(core))
    blocks = in_blocks(x, dim, sizes[0] * sizes[1])
    inside = blocks.shape[1:]
    blocks = blocks.reshape(*sizes, *inside).swapaxes(0, 1).reshape(-1, *inside)
    blocks = lax.psum_scatter(blocks, core, scatter_dimension=0, tiled=True)
    return lax.psum_scatter(blocks, chips, scatter_dimension=0, tiled=True)[0]


def sent_and_summed(x, axis, dim):
    blocks = in_blocks(x, dim, lax.axis_size(axis))
    arrived = lax.all_to_all(blocks, axis, split_axis=0, concat_axis=0, tiled=True)
    return arrived.sum(axis=0)


def one_axis_at_a_time(x, axes):
    for axis in axes:
        x = lax.psum(x, axis)
    return x


def contract(left, right):
    return lax.dot_general(
        left,
        right,
        (((0,), (0,)), ((), ())),
        precision=lax.Precision.HIGHEST,
        preferred_element_type=jnp.float32,
    )


def right_side(slab):
    return jnp.concatenate(
        [jnp.concatenate([slab[0], slab[1]], 1), jnp.concatenate([slab[1], -slab[0]], 1)], 0
    )


def defects(coef, block):
    square = 2.0 - block[0] * block[0] - block[1] * block[1]
    return jnp.dot(
        coef, square, precision=lax.Precision.HIGHEST, preferred_element_type=jnp.float32
    )


def body(matrix_elements, band_index, occupied, band_weight, coulomb):
    bands_dev = matrix_elements.shape[1]
    half = matrix_elements.shape[2]
    n_band = lax.axis_size(BAND)
    rows_dev = half // n_band
    factor = 1.0 / math.sqrt(bands_dev * n_band)
    occ = (band_index < occupied[0]).astype(jnp.float32)
    coef = (0.5 - occ) * band_weight
    slab = spread(matrix_elements[:, :, :COLS], "ga", 0)
    band_pos = lax.axis_index(BAND)
    ga_pos = lax.axis_index("ga")
    left = jnp.concatenate(
        [coef[:, None] * matrix_elements[0], coef[:, None] * matrix_elements[1]], 0
    )
    right = right_side(slab)
    sums = sum_by_chip(contract(left, right), ("band_0", "band_1", "band_2"), "band_3", 0)
    defect_full = defects(coef, matrix_elements)
    defect_slab = defects(coef, slab)
    row_def = sent_and_summed(defect_full, BAND, 0)
    col_def = one_axis_at_a_time(defect_slab, BAND)
    sums = sums * factor
    row_def = row_def * factor
    col_def = col_def * factor
    row_coul = lax.dynamic_slice_in_dim(coulomb, ga_pos * half + band_pos * rows_dev, rows_dev, 0)
    weight = jnp.sqrt(row_coul[:, None] * coulomb[None, :COLS])
    part_re = weight * (sums[:, :COLS] + 0.5 * (row_def[:, None] + col_def[None, :]))
    part_im = weight * sums[:, COLS:]
    return jnp.stack([part_re, part_im], 1)


def solution(mesh):
    finer = Mesh(
        mesh.devices.reshape(4, 2, 4, 2, mesh.shape["ga"]),
        ("band_0", "band_1", "band_2", "band_3", "ga"),
    )
    in_specs = (P(None, BAND, "ga"), P(BAND), P(), P(BAND), P())
    out_specs = P(GA_BAND, None, None)
    return jax.shard_map(body, mesh=finer, in_specs=in_specs, out_specs=out_specs, check_vma=False)
```

profile of v0, /device:TPU:64, one launch (start us, length us, event | category | flops | bytes accessed | tf_op | source)
XLA Modules:
  0.0 369.5 jit_solution(3057454762529198475)
XLA Ops:
  6.5 0.0 all-reduce.2.cloned.1.call-start
  6.5 2.4 slice_select_fusion
  8.9 0.0 all-reduce.2.cloned.1.call-update
  8.9 0.0 reduce-scatter.3.cloned.1.call-start
  9.0 10.6 %fusion.27 = (f32[1,256,6144]{2,1,0:T(8,128)}, f32[1,256,6144]{2,1,0:T(8,128)}) fusion(f32[2,256,6144]{2,1,0:T(8,128)} %param.5), kind=kLoop, calls=%fused_computation.43 | loop fusion | bytes 25165824 | tf_op jit(solution)/shard_map/slice | solution.py:80
  20.3 6.7 %copy.17 = f32[1,256,6144]{1,2,0:T(8,128)} copy(f32[1,256,6144]{2,1,0:T(8,128)} %get-tuple-element.5) | data formatting | bytes 12582912
  26.9 0.0 copy-start.2
  26.9 0.0 copy-start.3
  26.9 6.7 %copy.18 = f32[1,256,6144]{1,2,0:T(8,128)} copy(f32[1,256,6144]{2,1,0:T(8,128)} %get-tuple-element.6) | data formatting | bytes 12582912
  33.6 0.0 copy-done.2
  33.6 0.0 copy-done.3
  33.6 11.6 %fusion.4 = (f32[256,6144]{0,1:T(8,128)}, f32[256,6144]{0,1:T(8,128)}, f32[256,6144]{0,1:T(8,128)}) fusion(f32[1,256,6144]{1,2,0:T(8,128)} %copy.18, f32[1,256,6144]{1,2,0:T(8,128)} %copy.17, f32[256]{0:T(256)S(1)} %fusion.23), kind=kLoop, calls=%fused_computation.6 | loop fusion | flops 9437184 | bytes 31458304 | tf_op jit(solution)/shard_map/sub | solution.py:62
  45.2 11.5 %all-reduce.2.cloned.1.call-done = f32[2,256,512]{2,1,0:T(8,128)} async-done(((f32[2,256,512]{2,1,0:T(8,128)}), f32[2,256,512]{2,1,0:T(8,128)}) %all-reduce.2.cloned.1.call-update) | async-done | bytes 1048592 | tf_op jit(solution)/shard_map/psum | solution.py:16
  56.7 1.1 fusion.26
  57.8 1.3 slice_bitcast_fusion.1
  59.1 45.8 %fusion = f32[6144,1024]{1,0:T(8,128)} fusion(f32[256,6144]{0,1:T(8,128)} %get-tuple-element.9, f32[256,6144]{0,1:T(8,128)} %get-tuple-element.8, f32[256,512]{1,0:T(8,128)S(1)} %fusion.26, f32[256,512]{1,0:T(8,128)S(1)} %get-tuple-element.11, f32[256,512]{1,0:T(8,128)S(1)} %get-tuple-element.10), kind=kOutput, calls=%fused_computation | convolution fusion | flops 38659424256 | bytes 39321600 | tf_op jit(solution)/shard_map/dot_general | solution.py:46
  104.9 17.7 %copy.14 = f32[2,32,96,1024]{3,2,1,0:T(8,128)} copy(f32[2,32,96,1024]{3,2,0,1:T(8,128)} %bitcast.49) | data formatting | bytes 50331648 | tf_op jit(solution)/shard_map/transpose | solution.py:28
  122.6 0.0 reduce-scatter.3.cloned.1.call-update
  122.6 0.0 reduce-scatter.5.cloned.1.call-start
  122.6 41.9 %reduce-scatter.3.cloned.1.call-done = f32[32,96,1024]{2,1,0:T(8,128)} async-done(((f32[64,96,1024]{2,1,0:T(8,128)}), f32[32,96,1024]{2,1,0:T(8,128)}) %reduce-scatter.3.cloned.1.call-update) | async-done | bytes 12582928 | tf_op jit(solution)/shard_map/reduce_scatter | solution.py:29
  164.5 0.0 reduce-scatter.5.cloned.1.call-update
  164.5 0.0 copy-start.1
  164.5 0.0 copy-start
  164.6 0.0 slice-start
  164.6 14.4 %convolution_bitcast_fusion = f32[64,1,96]{2,1,0:T(1,128)} fusion(f32[256,1,1]{0,1,2:T(1,128)S(1)} %bitcast.52, f32[64,96,256]{2,1,0:T(8,128)} %bitcast.51), kind=kOutput, calls=%fused_computation.17 | convolution fusion | flops 18874368 | bytes 6317056 | tf_op jit(solution)/shard_map/dot_general | solution.py:63
  179.0 8.4 %all-to-all-start = ((f32[64,1,96]{2,1,0:T(1,128)}), f32[64,1,96]{2,1,0:T(1,128)S(1)}, u32[]{:S(2)}, u32[]{:S(2)}) async-start(f32[64,1,96]{2,1,0:T(1,128)} %convolution_bitcast_fusion), calls=%async_computation.2 | async-start | bytes 65536 | tf_op jit(solution)/shard_map/all_to_all | solution.py:35
  187.4 0.0 copy-done.1
  187.4 0.1 dynamic_slice.3
  187.5 8.0 %all-to-all-done = f32[64,1,96]{2,1,0:T(1,128)S(1)} async-done(((f32[64,1,96]{2,1,0:T(1,128)}), f32[64,1,96]{2,1,0:T(1,128)S(1)}, u32[]{:S(2)}, u32[]{:S(2)}) %all-to-all-start) | async-done | bytes 24608 | tf_op jit(solution)/shard_map/all_to_all | solution.py:35
  195.6 0.1 reduce_sum.9
  195.6 0.0 copy-done
  195.6 0.4 fusion.13
  196.1 8.6 %psum.36 = f32[512]{0:T(512)S(1)} all-reduce(f32[512]{0:T(512)S(1)} %bitcast.54), channel_id=1, replica_groups=mesh['band_0'=4,'band_1'=2,'band_2'=4,'band_3'=2,'ga'=2] {'band_0'}, use_global_device_ids=true, to_apply=%region_4.5 | all-reduce | flops 512 | bytes 4096 | tf_op jit(solution)/shard_map/psum | solution.py:41
  204.7 5.3 %psum.37 = f32[512]{0:T(512)S(1)} all-reduce(f32[512]{0:T(512)S(1)} %psum.36), channel_id=1, replica_groups=mesh['band_0'=4,'band_1'=2,'band_2'=4,'band_3'=2,'ga'=2] {'band_1'}, use_global_device_ids=true, to_apply=%region_5.6 | all-reduce | flops 512 | bytes 4096 | tf_op jit(solution)/shard_map/psum | solution.py:41
  210.0 11.4 %psum.38 = f32[512]{0:T(512)S(1)} all-reduce(f32[512]{0:T(512)S(1)} %psum.37), channel_id=1, replica_groups=mesh['band_0'=4,'band_1'=2,'band_2'=4,'band_3'=2,'ga'=2] {'band_2'}, use_global_device_ids=true, to_apply=%region_6.7 | all-reduce | flops 512 | bytes 4096 | tf_op jit(solution)/shard_map/psum | solution.py:41
  221.4 2.5 psum.39
  223.8 136.9 %reduce-scatter.5.cloned.1.call-done = f32[1,96,1024]{2,1,0:T(8,128)} async-done(((f32[32,96,1024]{2,1,0:T(8,128)}), f32[1,96,1024]{2,1,0:T(8,128)}) %reduce-scatter.5.cloned.1.call-update) | async-done | bytes 393232 | tf_op jit(solution)/shard_map/reduce_scatter | solution.py:30
  360.7 1.0 multiply_bitcast_fusion
  361.7 0.0 slice-done
  361.7 0.2 fusion.21
  361.9 1.1 copy.15
  (4 shorter events, 0.0 us)
Async XLA Ops:
  6.5 50.2 %all-reduce.2.cloned.1.call-start = ((), (), s32[]{:S(2)}) async-start(), calls=%async_computation.3 | async-start | bytes 2097152 | tf_op jit(solution)/shard_map/psum | solution.py:16
  8.9 155.6 %reduce-scatter.3.cloned.1.call-start = ((), (), s32[]{:S(2)}) async-start(), calls=%async_computation.4 | async-start | bytes 37748736 | tf_op jit(solution)/shard_map/reduce_scatter | solution.py:29
  26.9 6.7 %copy-start.2 = (f32[256]{0:T(256)S(1)}, f32[256]{0:T(256)}, u32[]{:S(2)}) copy-start(f32[256]{0:T(256)} %param.8) | copy-start | bytes 3076
  26.9 6.7 %copy-start.3 = (s32[256]{0:T(256)S(1)}, s32[256]{0:T(256)}, u32[]{:S(2)}) copy-start(s32[256]{0:T(256)} %param.6) | copy-start | bytes 3076
  122.6 238.1 %reduce-scatter.5.cloned.1.call-start = ((), (), s32[]{:S(2)}) async-start(), calls=%async_computation.5 | async-start | bytes 12976128 | tf_op jit(solution)/shard_map/reduce_scatter | solution.py:30
  164.5 22.9 %copy-start.1 = (f32[12288]{0:T(1024)S(1)}, f32[12288]{0:T(1024)}, u32[]{:S(2)}) copy-start(f32[12288]{0:T(1024)} %param.9) | copy-start | bytes 147460
  164.5 31.1 %copy-start = (f32[2,256,512]{2,1,0:T(8,128)S(1)}, f32[2,256,512]{2,1,0:T(8,128)}, u32[]{:S(2)}) copy-start(f32[2,256,512]{2,1,0:T(8,128)} %all-reduce.2.cloned.1.call-done) | copy-start | bytes 3145732
  164.6 197.2 %slice-start = ((f32[12288]{0:T(1024)}), f32[512]{0:T(512)S(1)}, s32[]{:S(2)}) async-start(f32[12288]{0:T(1024)} %param.9), calls=%async_computation.6 | async-start | bytes 4096 | tf_op jit(solution)/shard_map/slice | solution.py:92
  179.0 16.6 %all-to-all-start = ((f32[64,1,96]{2,1,0:T(1,128)}), f32[64,1,96]{2,1,0:T(1,128)S(1)}, u32[]{:S(2)}, u32[]{:S(2)}) async-start(f32[64,1,96]{2,1,0:T(1,128)} %convolution_bitcast_fusion), calls=%async_computation.2 | async-start | bytes 65536 | tf_op jit(solution)/shard_map/all_to_all | solution.py:35
Sparse Core Ops, SparseCore 0:
  9.8 46.9 all-reduce.1
  122.7 41.7 reduce-scatter.2
  166.9 193.7 reduce-scatter.4
where the time goes:
time: 370 us
  waiting for transfers between devices  198 us (54%)
  matrix products  60.6 us (16%)
  local copies, waits for them, and re-layouts  44.1 us (12%)
  blocking collectives  27.8 us (8%)
  other arithmetic  16.3 us (4%)
  between operations  13.9 us (4%)
  starting transfers between devices  8.52 us (2%)
    reduce_scatter x1, waiting for transfers between devices, sum_by_chip(): return lax.psum_scatter(blocks, chips, scatter_dimension=0, tiled=True)[0]  137 us
    dot_general x1, matrix products, contract(): lax.dot_general(left, right, (((0,), (0,)), ((), ())), precision=lax.Prec...  45.8 us
    reduce_scatter x1, waiting for transfers between devices, sum_by_chip(): blocks = lax.psum_scatter(blocks, core, scatter_dimension=0, tiled=True)  41.9 us
    psum x4, blocking collectives, one_axis_at_a_time(): x = lax.psum(x, axis)  27.8 us
    transpose x1, local copies, waits for them, and re-layouts, sum_by_chip(): blocks = blocks.reshape(*sizes, *inside).swapaxes(0, 1).reshape(-1, *inside)  17.7 us
    dot_general x2, matrix products, defects(): jnp.dot(coef, square, precision=lax.Precision.HIGHEST, preferred_element_...  14.8 us
    unnamed x10, local copies, waits for them, and re-layouts  13.4 us
    sub x1, other arithmetic, defects(): square = 2.0 - block[0] * block[0] - block[1] * block[1]  11.6 us
  transfers between devices with their start and end apart: 4, of which 4 were waited for; matrix products, arithmetic and copies ran while one was open for 14% of the time, Pallas kernels for 0%

commit v1 on v0

v1 whole, which is shorter than its diff:
```python
import functools
import math

import jax
import jax.numpy as jnp
from jax import lax
from jax.experimental import pallas as pl
from jax.experimental.pallas import tpu as pltpu
from jax.sharding import Mesh
from jax.sharding import PartitionSpec as P

COLS = 512
LANES = 128
BAND = ("band_0", "band_1", "band_2", "band_3")
GA_BAND = ("ga", "band_0", "band_1", "band_2", "band_3")
MESH = pl.DeviceIdType.MESH
RING = 4
ROUNDS = 8
F32 = jnp.float32
BF16 = jnp.bfloat16


def split(x):
    hi = x.astype(BF16)
    return hi, (x - hi.astype(F32)).astype(BF16)


def kernel(
    m_ref, bi_ref, bw_ref, occ_ref, o_ref,
    at, wst, rdef, cdef, coef, stage, slab, psend, pin,
    q, t1in, din, r1, t1in2, din2, r2, zin,
    stage_sem, slab_send, slab_sem, pair_send, pair_recv,
    t1_send, t1_recv, dr_send, dr_recv, cb_send, cb_recv,
    t1_send2, t1_recv2, dr_send2, dr_recv2, cb_send2, cb_recv2,
    z_send, z_recv,
):
    rows = o_ref.shape[0]
    half = rows // 2
    nb = m_ref.shape[1]
    group = 2 * RING * rows
    y, z, x, core, ga = (lax.axis_index(name) for name in ("band_0", "band_1", "band_2", "band_3", "ga"))
    up = lambda i: lax.rem(i + 1, RING)
    down = lambda i: lax.rem(i + RING - 1, RING)
    opposite = lambda i: lax.rem(i + 2, RING)

    barrier = pltpu.get_barrier_semaphore()
    peers = (
        {"band_3": 1 - core},
        {"band_2": up(x)},
        {"band_2": down(x)},
        {"band_0": up(y)},
        {"band_0": down(y)},
        {"band_1": 1 - z},
        {"ga": 1 - ga},
    )

    def stage_copy(i):
        zd, yy = i // RING, lax.rem(i, RING)
        start = pl.multiple_of((2 * yy + zd) * group, LANES)
        return pltpu.make_async_copy(
            m_ref.at[:, :, pl.ds(start, group)], stage.at[lax.rem(i, 2)], stage_sem.at[lax.rem(i, 2)]
        )

    def slab_local(j):
        return pltpu.make_async_copy(m_ref.at[:, :, pl.ds(j * LANES, LANES)], slab.at[j], slab_sem.at[j])

    def slab_remote(j):
        return pltpu.make_async_remote_copy(
            m_ref.at[:, :, pl.ds(j * LANES, LANES)], slab.at[j], slab_send.at[j], slab_sem.at[j],
            device_id={"ga": 1 - ga}, device_id_type=MESH,
        )

    stage_copy(jnp.int32(0)).start()
    stage_copy(jnp.int32(1)).start()

    for peer in peers:
        pl.semaphore_signal(barrier, inc=1, device_id=peer, device_id_type=MESH)
    pl.semaphore_wait(barrier, len(peers))

    @pl.when(ga == 0)
    def _():
        for j in range(COLS // LANES):
            slab_remote(j).start()
        for j in range(COLS // LANES):
            slab_local(j).start()

    c_row = (0.5 - (bi_ref[...] < occ_ref[0]).astype(F32)) * bw_ref[...]
    for i in range(nb // LANES):
        piece = c_row[:, i * LANES : (i + 1) * LANES]
        coef[pl.ds(i * LANES, LANES), :] = jnp.broadcast_to(piece, (LANES, LANES)).T

    def prep(i):
        zd, yy = i // RING, lax.rem(i, RING)
        slot = lax.rem(i, 2)
        stage_copy(i).wait()
        base = (2 * yy + zd) * group

        def column(k, carry):
            lanes = pl.ds(pl.multiple_of(k * LANES, LANES), LANES)
            here = pl.ds(pl.multiple_of(base + k * LANES, LANES), LANES)
            a = stage[slot, 0, :, lanes]
            b = stage[slot, 1, :, lanes]
            a_hi, a_lo = split(a)
            b_hi, b_lo = split(b)
            at[here, 0:nb] = a_hi.T
            at[here, nb : 2 * nb] = b_hi.T
            at[here, 2 * nb : 3 * nb] = a_lo.T
            at[here, 3 * nb : 4 * nb] = b_lo.T
            part = 0.5 * jnp.sum(coef[...] * (2.0 - a * a - b * b), axis=0, keepdims=True)
            rdef[here, :] = jnp.broadcast_to(part, (LANES, LANES)).T
            return carry

        lax.fori_loop(0, group // LANES, column, 0)

        @pl.when(i + 2 < 2 * RING)
        def _():
            stage_copy(i + 2).start()

    def weights(j):
        @pl.when(ga == 0)
        def _():
            slab_local(j).wait()

        @pl.when(ga == 1)
        def _():
            slab_remote(j).wait_recv()

        a = slab[j, 0]
        b = slab[j, 1]
        c = coef[...]
        cdef[...] = 0.5 * jnp.sum(c * (2.0 - a * a - b * b), axis=0, keepdims=True)
        a_hi, a_lo = split(c * a)
        b_hi, b_lo = split(c * b)
        for at_row, aa, bb in ((0, a_hi, b_hi), (2 * nb, a_hi, b_hi), (4 * nb, a_lo, b_lo)):
            wst[at_row : at_row + nb, 0:LANES] = aa
            wst[at_row : at_row + nb, LANES:] = bb
            wst[at_row + nb : at_row + 2 * nb, 0:LANES] = bb
            wst[at_row + nb : at_row + 2 * nb, LANES:] = -aa

    def product(yy, zd, parity):
        base = (2 * yy + zd) * group + parity * rows
        spots = [pl.ds(pl.multiple_of(base + 2 * xx * rows, 16), rows) for xx in range(RING)]
        left = jnp.concatenate([at[s, :] for s in spots], 0)
        left = jnp.concatenate([left, left[:, : 2 * nb]], 1)
        out = jnp.dot(left, wst[...], preferred_element_type=F32)
        shift = jnp.concatenate([rdef[s, :] for s in spots], 0) + cdef[...]
        return out[:, :LANES] + shift, out[:, LANES:]

    def pair_copy(r, yy):
        return pltpu.make_async_remote_copy(
            psend.at[lax.rem(r, 2), yy], pin.at[r, yy], pair_send.at[r, yy], pair_recv.at[r, yy],
            device_id={"band_3": 1 - core}, device_id_type=MESH,
        )

    first = (0, half)
    second = (half, half)

    class Stage:
        def __init__(self, held, slots, tin, landed, sems, axes):
            self.held, self.slots, self.tin, self.landed = held, slots, tin, landed
            self.sems, self.axes = sems, axes

        def chunk(self, r, k, d, part):
            return self.held.at[lax.rem(r, self.slots), k, d, :, pl.ds(*part), :]

        def send(self, which, r, k, way):
            name, me = self.axes[k]
            to = up(me) if way == 0 else down(me)
            mine, other = (first, second) if way == 0 else (second, first)
            if which == 0:
                src, dst = self.chunk(r, k, opposite(me), mine), self.tin.at[r, k, way]
            elif which == 1:
                src, dst = self.chunk(r, k, to, other), self.landed.at[r, k, way, :, pl.ds(*other), :]
            else:
                src, dst = self.chunk(r, k, to, mine), self.landed.at[r, k, way, :, pl.ds(*mine), :]
            ss, rs = self.sems[which]
            return pltpu.make_async_remote_copy(
                src, dst, ss.at[r, k, way], rs.at[r, k, way], device_id={name: to}, device_id_type=MESH
            )

        def begin(self, r):
            for which in (0, 1):
                for k in range(2):
                    for way in range(2):
                        self.send(which, r, k, way).start()

        def combine(self, r):
            slot = lax.rem(r, self.slots)
            for k in range(2):
                me = self.axes[k][1]
                for way in range(2):
                    to = up(me) if way == 0 else down(me)
                    mine = pl.ds(*(first if way == 0 else second))
                    self.send(0, r, k, way).wait_recv()
                    self.held[slot, k, to, :, mine, :] += self.tin[r, k, way]
                    self.send(2, r, k, way).start()

        def arrived(self, r):
            for which in (1, 2):
                for k in range(2):
                    for way in range(2):
                        self.send(which, r, k, way).wait_recv()

        def total(self, r, k):
            return self.held[lax.rem(r, self.slots), k, self.axes[k][1]] + self.landed[r, k, 0] + self.landed[r, k, 1]

        def sent(self, r):
            for which in range(3):
                for k in range(2):
                    for way in range(2):
                        self.send(which, r, k, way).wait_send()

    one = Stage(
        q, 4, t1in, din, ((t1_send, t1_recv), (dr_send, dr_recv), (cb_send, cb_recv)),
        (("band_2", x), ("band_0", y)),
    )
    two = Stage(
        r1, 4, t1in2, din2, ((t1_send2, t1_recv2), (dr_send2, dr_recv2), (cb_send2, cb_recv2)),
        (("band_0", y), ("band_2", x)),
    )

    def z_copy(r):
        return pltpu.make_async_remote_copy(
            r2.at[lax.rem(r, 2)], zin.at[r], z_send.at[r], z_recv.at[r],
            device_id={"band_1": 1 - z}, device_id_type=MESH,
        )

    def step(r, carry):
        @pl.when(r < 2)
        def _():
            lax.fori_loop(0, RING, lambda yy, c: (prep(r * RING + yy), c)[1], 0)

        @pl.when(r < ROUNDS)
        def _():
            j, zd = r // 2, lax.rem(r, 2)

            @pl.when(zd == 0)
            def _():
                weights(j)

            def give(yy, c):
                @pl.when(r >= 2)
                def _():
                    pair_copy(r - 2, yy).wait_send()

                re, im = product(yy, zd, 1 - core)
                for xx in range(RING):
                    psend[lax.rem(r, 2), yy, 0, xx] = re[xx * rows : (xx + 1) * rows]
                    psend[lax.rem(r, 2), yy, 1, xx] = im[xx * rows : (xx + 1) * rows]
                pair_copy(r, yy).start()
                return c

            lax.fori_loop(0, RING, give, 0)

            def keep(yy, c):
                re, im = product(yy, zd, core)
                pair_copy(r, yy).wait_recv()
                slot = lax.rem(r, 4)
                for xx in range(RING):
                    q[slot, 0, xx, yy] = re[xx * rows : (xx + 1) * rows] + pin[r, yy, 0, xx]
                    q[slot, 1, yy, xx] = im[xx * rows : (xx + 1) * rows] + pin[r, yy, 1, xx]
                return c

            lax.fori_loop(0, RING, keep, 0)
            one.begin(r)

        @pl.when((r >= ROUNDS) & (r < ROUNDS + 2))
        def _():
            lax.fori_loop(0, RING, lambda yy, c: (pair_copy(r - 2, yy).wait_send(), c)[1], 0)

        @pl.when((r >= 1) & (r < ROUNDS + 1))
        def _():
            one.combine(r - 1)

        @pl.when((r >= 2) & (r < ROUNDS + 2))
        def _():
            t = r - 2
            one.arrived(t)
            for k in range(2):
                r1[lax.rem(t, 4), k, :, 0] = one.total(t, k)
            two.begin(t)

        @pl.when((r >= 3) & (r < ROUNDS + 3))
        def _():
            two.combine(r - 3)
            one.sent(r - 3)

        @pl.when((r >= 4) & (r < ROUNDS + 4))
        def _():
            t = r - 4
            two.arrived(t)
            for k in range(2):
                r2[lax.rem(t, 2), k] = two.total(t, k)[0]

            @pl.when(lax.rem(t, 2) != z)
            def _():
                z_copy(t).start()

        @pl.when(r >= 5)
        def _():
            t = r - 5
            two.sent(t)

            @pl.when(lax.rem(t, 2) != z)
            def _():
                z_copy(t).wait_send()

            @pl.when(lax.rem(t, 2) == z)
            def _():
                z_copy(t).wait_recv()
                for k in range(2):
                    spot = pl.ds(pl.multiple_of(k * COLS + (t // 2) * LANES, LANES), LANES)
                    o_ref[:, spot] = r2[lax.rem(t, 2), k] + zin[t, k]

        return carry

    lax.fori_loop(0, ROUNDS + 5, step, 0)

    @pl.when(ga == 0)
    def _():
        for j in range(COLS // LANES):
            slab_remote(j).wait_send()


def sums_of(matrix_elements, band_index, band_weight, occupied):
    nb, ng = matrix_elements.shape[1:]
    rows = ng // (2 * RING * RING * 2)
    half = rows // 2
    group = 2 * RING * rows
    dma = pltpu.SemaphoreType.DMA
    quad = lambda: [dma((ROUNDS, 2, 2)) for _ in range(6)]
    vmem = pl.BlockSpec(memory_space=pltpu.VMEM)
    return pl.pallas_call(
        kernel,
        out_shape=jax.ShapeDtypeStruct((rows, 2 * COLS), F32),
        in_specs=[pl.BlockSpec(memory_space=pl.ANY), vmem, vmem, pl.BlockSpec(memory_space=pltpu.SMEM)],
        out_specs=vmem,
        scratch_shapes=[
            pltpu.VMEM((ng, 4 * nb), BF16),
            pltpu.VMEM((6 * nb, 2 * LANES), BF16),
            pltpu.VMEM((ng, LANES), F32),
            pltpu.VMEM((1, LANES), F32),
            pltpu.VMEM((nb, LANES), F32),
            pltpu.VMEM((2, 2, nb, group), F32),
            pltpu.VMEM((COLS // LANES, 2, nb, LANES), F32),
            pltpu.VMEM((2, RING, 2, RING, rows, LANES), F32),
            pltpu.VMEM((ROUNDS, RING, 2, RING, rows, LANES), F32),
            pltpu.VMEM((4, 2, RING, RING, rows, LANES), F32),
            pltpu.VMEM((ROUNDS, 2, 2, RING, half, LANES), F32),
            pltpu.VMEM((ROUNDS, 2, 2, RING, rows, LANES), F32),
            pltpu.VMEM((4, 2, RING, 1, rows, LANES), F32),
            pltpu.VMEM((ROUNDS, 2, 2, 1, half, LANES), F32),
            pltpu.VMEM((ROUNDS, 2, 2, 1, rows, LANES), F32),
            pltpu.VMEM((2, 2, rows, LANES), F32),
            pltpu.VMEM((ROUNDS, 2, rows, LANES), F32),
            dma((2,)), dma((COLS // LANES,)), dma((COLS // LANES,)),
            dma((ROUNDS, RING)), dma((ROUNDS, RING)),
            *quad(), *quad(),
            dma((ROUNDS,)), dma((ROUNDS,)),
        ],
        compiler_params=pltpu.CompilerParams(
            collective_id=0, has_side_effects=True, vmem_limit_bytes=67043328
        ),
        name="remainder_sums",
    )(matrix_elements, band_index.reshape(1, nb), band_weight.reshape(1, nb), occupied)


def body(matrix_elements, band_index, occupied, band_weight, coulomb):
    bands_dev, half = matrix_elements.shape[1:]
    n_band = lax.axis_size(BAND)
    rows_dev = half // n_band
    factor = 1.0 / math.sqrt(bands_dev * n_band)
    sums = sums_of(matrix_elements, band_index, band_weight, occupied)
    start = lax.axis_index("ga") * half + lax.axis_index(BAND) * rows_dev
    row_coul = lax.dynamic_slice_in_dim(coulomb, start, rows_dev, 0)
    weight = jnp.sqrt(row_coul[:, None] * coulomb[None, :COLS])
    return sums.reshape(rows_dev, 2, COLS) * factor * weight[:, None, :]


def solution(mesh):
    finer = Mesh(
        mesh.devices.reshape(4, 2, 4, 2, mesh.shape["ga"]),
        ("band_0", "band_1", "band_2", "band_3", "ga"),
    )
    in_specs = (P(None, BAND, "ga"), P(BAND), P(), P(BAND), P())
    out_specs = P(GA_BAND, None, None)
    return jax.shard_map(body, mesh=finer, in_specs=in_specs, out_specs=out_specs, check_vma=False)
```

time: 370 us -> 105 us (0.28)
  waiting for transfers between devices: 198 us -> 0 us
  Pallas kernels: 0 us -> 99 us
  matrix products: 60.6 us -> 0 us
  local copies, waits for them, and re-layouts: 44.1 us -> 2.78 us
  blocking collectives: 27.8 us -> 0 us
  other arithmetic: 16.3 us -> 1.08 us
  between operations: 13.9 us -> 0.67 us
  starting transfers between devices: 8.52 us -> 0 us
    reduce_scatter x2 -> x0, waiting for transfers between devices: 179 us -> none  [the longest x1 137 us: sum_by_chip(): return lax.psum_scatter(blocks, chips, scatter_dimension=0, tiled=True)[0]]
    pallas_call x0 -> x1, Pallas kernels: none -> 99 us  [sums_of(): pl.pallas_call(kernel, out_shape=jax.ShapeDtypeStruct((rows, 2 * COLS), F...]
    dot_general x3 -> x0, matrix products: 60.6 us -> none  [the longest x1 45.8 us: contract(): lax.dot_general(left, right, (((0,), (0,)), ((), ())), precision=lax.Prec...]
    psum x4 -> x0, blocking collectives: 27.8 us -> none  [one_axis_at_a_time(): x = lax.psum(x, axis)]
    transpose x1 -> x0, local copies, waits for them, and re-layouts: 17.7 us -> none  [sum_by_chip(): blocks = blocks.reshape(*sizes, *inside).swapaxes(0, 1).reshape(-1, *inside)]
    unnamed x10 -> x0, local copies, waits for them, and re-layouts: 13.4 us -> none
    sub x1 -> x0, other arithmetic: 11.6 us -> none  [defects(): square = 2.0 - block[0] * block[0] - block[1] * block[1]]
    psum x1 -> x0, waiting for transfers between devices: 11.5 us -> none  [spread(): return lax.psum(jnp.where(mine, x, jnp.zeros_like(x)), axis)]
  transfers between devices with their start and end apart: 4 -> 0, of which waited for: 4 -> 0; matrix products, arithmetic and copies ran while one was open for 14% -> 0% of each run, Pallas kernels for 0% -> 0%
where the time goes in v1:
time: 105 us; the launch traced here: 104 us
  Pallas kernels  99 us (94%)
  local copies, waits for them, and re-layouts  2.78 us (3%)
  other arithmetic  1.08 us (1%)
    pallas_call x1, Pallas kernels, sums_of(): pl.pallas_call(kernel, out_shape=jax.ShapeDtypeStruct((rows, 2 * COLS), F...  99 us

profile of v1, /device:TPU:64, one launch (start us, length us, event | category | flops | bytes accessed | tf_op | source)
XLA Modules:
  0.0 103.5 jit_solution(9019307217896926641)
XLA Ops:
  0.7 99.0 %remainder_sums.1 = f32[96,1024]{1,0:T(8,128)} custom-call(f32[2,256,6144]{2,1,0:T(8,128)} %m_ref.1, s32[1,256]{1,0:T(1,128)} %bitcast.2, f32[1,256]{1,0:T(1,128)} %bitcast.3, s32[1]{0:T(128)S(6)} %copy.6.occ_ref), custom_call_target="tpu_custom_call" | custom-call | tf_op jit(solution)/shard_map/remainder_sums/pallas_call | solution.py:333
  99.6 1.3 %reshape.35 = f32[96,2,512]{2,1,0:T(2,128)S(1)} reshape(f32[96,1024]{1,0:T(8,128)} %remainder_sums.1) | data formatting | bytes 786432 | tf_op jit(solution)/shard_map/reshape | solution.py:377
  101.0 0.7 slice.3
  101.7 0.8 dynamic_slice.3
  102.4 0.1 sqrt_multiply_fusion
  102.6 0.9 broadcast_multiply_fusion

commit v2 on v0

v2 whole, which is shorter than its diff:
```python
import functools
import math

import jax
import jax.numpy as jnp
from jax import lax
from jax.experimental import pallas as pl
from jax.experimental.pallas import tpu as pltpu
from jax.sharding import Mesh
from jax.sharding import PartitionSpec as P

COLS = 512
LANES = 128
BAND = ("band_0", "band_1", "band_2", "band_3")
GA_BAND = ("ga", "band_0", "band_1", "band_2", "band_3")
MESH = pl.DeviceIdType.MESH
Z_ORDER = (2, 3, 1, 0)
RING = 4
PARTS = 2
ROUNDS = 4 * PARTS
LAGS = (1, 2, 3, 4, 5)
SLOTS = 4
STAGES = 4
F32 = jnp.float32
BF16 = jnp.bfloat16


def split(x):
    hi = x.astype(BF16)
    return hi, (x - hi.astype(F32)).astype(BF16)


def kernel(
    m_ref, bi_ref, bw_ref, coul_ref, occ_ref, o_ref,
    at, wst, rdef, cdef, coef, rowc, stage, slab, psend, pin,
    q, t1in, din, r1, zin, rz, t1in2, din2,
    stage_sem, slab_copy, slab_send, slab_recv, pair_send, pair_recv,
    t1_send, t1_recv, in_send, in_recv, t1_send2, t1_recv2, in_send2, in_recv2,
    z_send, z_recv,
):
    rows = o_ref.shape[0]
    part = rows // PARTS
    nb = m_ref.shape[1]
    ng = m_ref.shape[2]
    n_chunks = COLS // LANES
    scale = 1.0 / math.sqrt(nb * 2 * RING * RING * 2)
    group = 2 * RING * rows
    y, z, x, core, ga = (lax.axis_index(name) for name in ("band_0", "band_1", "band_2", "band_3", "ga"))
    up = lambda i: lax.rem(i + 1, RING)
    down = lambda i: lax.rem(i + RING - 1, RING)
    opposite = lambda i: lax.rem(i + 2, RING)

    barrier = pltpu.get_barrier_semaphore()
    peers = (
        {"ga": 1 - ga},
        {"band_2": up(x)},
        {"band_2": down(x)},
        {"band_0": up(y)},
        {"band_0": down(y)},
        {"band_1": 1 - z},
        {"band_3": 1 - core},
    )
    for peer in peers:
        pl.semaphore_signal(barrier, inc=1, device_id=peer, device_id_type=MESH)

    def stage_copy(i):
        start = pl.multiple_of(i * group, LANES)
        return pltpu.make_async_copy(
            m_ref.at[:, :, pl.ds(start, group)], stage.at[lax.rem(i, STAGES)], stage_sem.at[lax.rem(i, STAGES)]
        )

    def size_of(ref, send_sem, recv_sem):
        return pltpu.make_async_remote_copy(
            ref, ref, send_sem, recv_sem, device_id={"band_3": 1 - core}, device_id_type=MESH
        )

    def slab_local(j):
        return pltpu.make_async_copy(m_ref.at[:, :, pl.ds(j * LANES, LANES)], slab.at[j], slab_copy.at[0])

    def slab_remote(j):
        return pltpu.make_async_remote_copy(
            slab.at[j], slab.at[j], slab_send.at[0], slab_recv.at[j],
            device_id={"ga": 1 - ga}, device_id_type=MESH,
        )

    @pl.when(ga == 0)
    def _():
        for j in range(n_chunks):
            slab_local(j).start()

    for i in range(STAGES):
        stage_copy(jnp.int32(i)).start()

    c_row = (0.5 - (bi_ref[...] < occ_ref[0]).astype(F32)) * bw_ref[...]
    for i in range(nb // LANES):
        piece = c_row[:, i * LANES : (i + 1) * LANES]
        coef[pl.ds(i * LANES, LANES), :] = jnp.broadcast_to(piece, (LANES, LANES)).T

    total_g = coul_ref.shape[1]
    row_start = ga * ng + (((y * 2 + z) * RING + x) * 2 + core) * rows
    block = (row_start // LANES) * LANES
    after = lax.rem(block + LANES, total_g)
    window = jnp.concatenate(
        [coul_ref[:, pl.ds(pl.multiple_of(b, LANES), LANES)] for b in (block, after)], 1
    )
    window = pltpu.roll(jnp.broadcast_to(window, (8, 2 * LANES)), lax.rem(2 * LANES - (row_start - block), 2 * LANES), 1)
    rowc[...] = jnp.broadcast_to(window[:1, :LANES], (LANES, LANES)).T

    def prep(i, carry):
        slot = lax.rem(i, STAGES)
        stage_copy(i).wait()

        def column(k, carry):
            lanes = pl.ds(pl.multiple_of(k * LANES, LANES), LANES)
            here = pl.ds(pl.multiple_of(i * group + k * LANES, LANES), LANES)
            a = stage[slot, 0, :, lanes]
            b = stage[slot, 1, :, lanes]
            a_hi, a_lo = split(a)
            b_hi, b_lo = split(b)
            at[here, 0:nb] = a_hi.T
            at[here, nb : 2 * nb] = b_hi.T
            at[here, 2 * nb : 3 * nb] = a_lo.T
            at[here, 3 * nb : 4 * nb] = b_lo.T
            share = 0.5 * jnp.sum(coef[...] * (2.0 - a * a - b * b), axis=0, keepdims=True)
            rdef[here, :] = jnp.broadcast_to(share, (LANES, LANES)).T
            return carry

        lax.fori_loop(0, group // LANES, column, 0)

        @pl.when(i + STAGES < 2 * RING)
        def _():
            stage_copy(i + STAGES).start()

        return carry

    prep(jnp.int32(0), 0)

    @pl.when(ga == 0)
    def _():
        pltpu.make_async_copy(slab, slab, slab_copy.at[0]).wait()

    pl.semaphore_wait(barrier, len(peers))

    @pl.when(ga == 0)
    def _():
        for j in range(n_chunks):
            slab_remote(j).start()

    lax.fori_loop(1, 2 * RING, prep, 0)

    def weights(j):
        @pl.when(ga == 1)
        def _():
            slab_remote(j).wait_recv()

        w = lax.rem(j, 2)
        a = slab[j, 0]
        b = slab[j, 1]
        c = coef[...]
        cdef[w] = 0.5 * jnp.sum(c * (2.0 - a * a - b * b), axis=0, keepdims=True)
        a_hi, a_lo = split(c * a)
        b_hi, b_lo = split(c * b)
        for at_row, aa, bb in ((0, a_hi, b_hi), (2 * nb, a_hi, b_hi), (4 * nb, a_lo, b_lo)):
            wst[w, at_row : at_row + nb, 0:LANES] = aa
            wst[w, at_row : at_row + nb, LANES:] = bb
            wst[w, at_row + nb : at_row + 2 * nb, 0:LANES] = bb
            wst[w, at_row + nb : at_row + 2 * nb, LANES:] = -aa

    pieces = [(y2, zd, xx) for y2 in range(2) for zd in range(2) for xx in range(RING)]

    def product(r, g, parity):
        w = lax.rem(r // PARTS, 2)
        base = g * (4 * group) + parity * rows + lax.rem(r, PARTS) * part
        spots = [
            pl.ds(pl.multiple_of(base + (2 * y2 + zd) * group + 2 * xx * rows, 16), part)
            for y2, zd, xx in pieces
        ]
        left = jnp.concatenate([at[s, :] for s in spots], 0)
        left = jnp.concatenate([left, left[:, : 2 * nb]], 1)
        out = jnp.dot(left, wst[w], preferred_element_type=F32)
        shift = jnp.concatenate([rdef[s, :] for s in spots], 0) + cdef[w]
        return out[:, :LANES] + shift, out[:, LANES:]

    def pair_copy(r, g):
        return pltpu.make_async_remote_copy(
            psend.at[lax.rem(r, 2), g], pin.at[r, g], pair_send.at[lax.rem(r, 2), g], pair_recv.at[r, g],
            device_id={"band_3": 1 - core}, device_id_type=MESH,
        )

    def give(r):
        @pl.when(lax.rem(r, PARTS) == 0)
        def _():
            weights(r // PARTS)

        def one_pair(g, carry):
            @pl.when(r >= 2)
            def _():
                pair_copy(r - 2, g).wait_send()

            re, im = product(r, g, 1 - core)
            for n, (y2, zd, xx) in enumerate(pieces):
                psend[lax.rem(r, 2), g, 0, zd, y2, xx] = re[n * part : (n + 1) * part]
                psend[lax.rem(r, 2), g, 1, zd, y2, xx] = im[n * part : (n + 1) * part]
            pair_copy(r, g).start()
            return carry

        lax.fori_loop(0, 2, one_pair, 0)

    def keep(r):
        slot = lax.rem(r, SLOTS)

        def one_pair(g, carry):
            re, im = product(r, g, core)
            pair_copy(r, g).wait_recv()
            for n, (y2, zd, xx) in enumerate(pieces):
                q[slot, 0, xx, zd, 2 * g + y2] = re[n * part : (n + 1) * part] + pin[r, g, 0, zd, y2, xx]
                q[slot, 1, 2 * g + y2, zd, xx] = im[n * part : (n + 1) * part] + pin[r, g, 1, zd, y2, xx]
            return carry

        lax.fori_loop(0, 2, one_pair, 0)

    class Stage:
        def __init__(self, held, tin, landed, cut, sems, axes):
            self.held, self.tin, self.landed = held, tin, landed
            self.cut, self.sems, self.axes = cut, sems, axes

        def send(self, which, r, k, way):
            name, me = self.axes[k]
            to = up(me) if way == 0 else down(me)
            here = self.cut(way if which != 1 else 1 - way)
            chunk = (lax.rem(r, SLOTS), k, opposite(me) if which == 0 else to)
            src = self.held.at[chunk + here]
            dst = self.tin.at[r, k, way] if which == 0 else self.landed.at[(r, k, way) + here]
            ss, rs = self.sems[min(which, 1)]
            return pltpu.make_async_remote_copy(
                src, dst, ss.at[lax.rem(r, SLOTS)], rs.at[r], device_id={name: to}, device_id_type=MESH
            )

        def whole(self, which, r):
            ref = (self.tin if which == 0 else self.landed).at[r]
            ss, rs = self.sems[which]
            return size_of(ref, ss.at[lax.rem(r, SLOTS)], rs.at[r])

        def begin(self, r, which, k):
            for way in range(2):
                self.send(which, r, k, way).start()

        def combine(self, r):
            self.whole(0, r).wait_recv()
            for k in range(2):
                me = self.axes[k][1]
                for way in range(2):
                    to = up(me) if way == 0 else down(me)
                    here = (lax.rem(r, SLOTS), k, to) + self.cut(way)
                    self.held[here] += self.tin[r, k, way]
                    self.send(2, r, k, way).start()

        def arrived(self, r):
            self.whole(1, r).wait_recv()

        def total(self, r, k):
            return self.held[lax.rem(r, SLOTS), k, self.axes[k][1]] + self.landed[r, k, 0] + self.landed[r, k, 1]

        def sent(self, r):
            self.whole(0, r).wait_send()
            self.whole(1, r).wait_send()

    along_x, along_y = ("band_2", x), ("band_0", y)
    one = Stage(
        q, t1in, din, lambda h: (h,),
        ((t1_send, t1_recv), (in_send, in_recv)), (along_x, along_y),
    )
    two = Stage(
        rz, t1in2, din2, lambda h: (pl.ds(h * (part // 2), part // 2),),
        ((t1_send2, t1_recv2), (in_send2, in_recv2)), (along_y, along_x),
    )

    def z_copy(r, k, m):
        e = lax.rem(two.axes[k][1] + Z_ORDER[m], RING)
        return pltpu.make_async_remote_copy(
            r1.at[lax.rem(r, SLOTS), k, 1 - z, e], zin.at[r, k, e],
            z_send.at[lax.rem(r, SLOTS), min(m, 1)], z_recv.at[r, min(m, 1)],
            device_id={"band_1": 1 - z}, device_id_type=MESH,
        )

    def z_whole(r, n):
        ref = zin.at[r, :, pl.ds(n, 1 + 2 * n)]
        return size_of(ref, z_send.at[lax.rem(r, SLOTS), n], z_recv.at[r, n])

    def to_other_z(t):
        one.arrived(t)
        for k in range(2):
            r1[lax.rem(t, SLOTS), k] = one.total(t, k)
        for m in range(RING):
            for k in range(2):
                z_copy(t, k, m).start()

    def from_other_z(t):
        slot = lax.rem(t, SLOTS)
        for which, ms in ((0, (0,)), (1, (1, 2, 3))):
            z_whole(t, which).wait_recv()
            for k in range(2):
                for m in ms:
                    e = lax.rem(two.axes[k][1] + Z_ORDER[m], RING)
                    rz[slot, k, e] = r1[slot, k, z, e] + zin[t, k, e]
                two.begin(t, which, k)
        one.sent(t)

    def second_combine(t):
        two.combine(t)
        for n in range(2):
            z_whole(t, n).wait_send()

    def finish(t):
        down_to = pl.ds(pl.multiple_of(lax.rem(t, PARTS) * part, 8), part)
        lanes = pl.multiple_of((t // PARTS) * LANES, LANES)
        weight = jnp.sqrt(rowc[down_to, :] * coul_ref[:, pl.ds(lanes, LANES)]) * scale
        two.arrived(t)
        for k in range(2):
            o_ref[down_to, k, pl.ds(lanes, LANES)] = two.total(t, k) * weight
        two.sent(t)

    give(jnp.int32(0))

    def step(r, carry):
        @pl.when(r + 1 < ROUNDS)
        def _():
            give(r + 1)

        @pl.when(r < ROUNDS)
        def _():
            keep(r)
            for which in (0, 1):
                for k in range(2):
                    one.begin(r, which, k)

        def late(lag, stage_work):
            @pl.when((r >= lag) & (r < ROUNDS + lag))
            def _():
                stage_work(r - lag)

        for lag, stage_work in zip(LAGS, (one.combine, to_other_z, from_other_z, second_combine, finish)):
            late(lag, stage_work)

        return carry

    lax.fori_loop(0, ROUNDS + LAGS[-1], step, 0)

    for g in range(2):
        pair_copy(ROUNDS - 2, g).wait_send()
        pair_copy(ROUNDS - 1, g).wait_send()

    @pl.when(ga == 0)
    def _():
        size_of(slab, slab_send.at[0], slab_recv.at[0]).wait_send()


def sums_of(matrix_elements, band_index, band_weight, coulomb, occupied):
    nb, ng = matrix_elements.shape[1:]
    rows = ng // (2 * RING * RING * 2)
    part = rows // PARTS
    group = 2 * RING * rows
    n_chunks = COLS // LANES
    dma = pltpu.SemaphoreType.DMA
    ring = lambda: [dma((n,)) for n in (SLOTS, ROUNDS, SLOTS, ROUNDS)]
    vmem = pl.BlockSpec(memory_space=pltpu.VMEM)
    return pl.pallas_call(
        kernel,
        out_shape=jax.ShapeDtypeStruct((rows, 2, COLS), F32),
        in_specs=[pl.BlockSpec(memory_space=pl.ANY), vmem, vmem, vmem, pl.BlockSpec(memory_space=pltpu.SMEM)],
        out_specs=vmem,
        scratch_shapes=[
            pltpu.VMEM((ng, 4 * nb), BF16),
            pltpu.VMEM((2, 6 * nb, 2 * LANES), BF16),
            pltpu.VMEM((ng, LANES), F32),
            pltpu.VMEM((2, 1, LANES), F32),
            pltpu.VMEM((nb, LANES), F32),
            pltpu.VMEM((LANES, LANES), F32),
            pltpu.VMEM((STAGES, 2, nb, group), F32),
            pltpu.VMEM((n_chunks, 2, nb, LANES), F32),
            pltpu.VMEM((2, 2, 2, 2, 2, RING, part, LANES), F32),
            pltpu.VMEM((ROUNDS, 2, 2, 2, 2, RING, part, LANES), F32),
            pltpu.VMEM((SLOTS, 2, RING, 2, RING, part, LANES), F32),
            pltpu.VMEM((ROUNDS, 2, 2, RING, part, LANES), F32),
            pltpu.VMEM((ROUNDS, 2, 2, 2, RING, part, LANES), F32),
            pltpu.VMEM((SLOTS, 2, 2, RING, part, LANES), F32),
            pltpu.VMEM((ROUNDS, 2, RING, part, LANES), F32),
            pltpu.VMEM((SLOTS, 2, RING, part, LANES), F32),
            pltpu.VMEM((ROUNDS, 2, 2, part // 2, LANES), F32),
            pltpu.VMEM((ROUNDS, 2, 2, part, LANES), F32),
            dma((STAGES,)), dma((1,)), dma((1,)), dma((n_chunks,)),
            dma((2, 2)), dma((ROUNDS, 2)),
            *ring(), *ring(),
            dma((SLOTS, 2)), dma((ROUNDS, 2)),
        ],
        compiler_params=pltpu.CompilerParams(
            collective_id=0, has_side_effects=True, vmem_limit_bytes=67043328
        ),
        name="remainder_sums",
    )(
        matrix_elements, band_index.reshape(1, nb), band_weight.reshape(1, nb),
        coulomb.reshape(1, -1), occupied,
    )


def body(matrix_elements, band_index, occupied, band_weight, coulomb):
    return sums_of(matrix_elements, band_index, band_weight, coulomb, occupied)


def solution(mesh):
    finer = Mesh(
        mesh.devices.reshape(4, 2, 4, 2, mesh.shape["ga"]),
        ("band_0", "band_1", "band_2", "band_3", "ga"),
    )
    in_specs = (P(None, BAND, "ga"), P(BAND), P(), P(BAND), P())
    out_specs = P(GA_BAND, None, None)
    return jax.shard_map(body, mesh=finer, in_specs=in_specs, out_specs=out_specs, check_vma=False)
```

time: 370 us -> 91.6 us (0.25)
  waiting for transfers between devices: 198 us -> 0 us
  Pallas kernels: 0 us -> 89 us
  matrix products: 60.6 us -> 0 us
  local copies, waits for them, and re-layouts: 44.1 us -> 1.77 us
  blocking collectives: 27.8 us -> 0 us
  other arithmetic: 16.3 us -> 0 us
  between operations: 13.9 us -> 0.66 us
  starting transfers between devices: 8.52 us -> 0 us
    reduce_scatter x2 -> x0, waiting for transfers between devices: 179 us -> none  [the longest x1 137 us: sum_by_chip(): return lax.psum_scatter(blocks, chips, scatter_dimension=0, tiled=True)[0]]
    pallas_call x0 -> x1, Pallas kernels: none -> 89 us  [sums_of(): pl.pallas_call(kernel, out_shape=jax.ShapeDtypeStruct((rows, 2, COLS), F3...]
    dot_general x3 -> x0, matrix products: 60.6 us -> none  [the longest x1 45.8 us: contract(): lax.dot_general(left, right, (((0,), (0,)), ((), ())), precision=lax.Prec...]
    psum x4 -> x0, blocking collectives: 27.8 us -> none  [one_axis_at_a_time(): x = lax.psum(x, axis)]
    transpose x1 -> x0, local copies, waits for them, and re-layouts: 17.7 us -> none  [sum_by_chip(): blocks = blocks.reshape(*sizes, *inside).swapaxes(0, 1).reshape(-1, *inside)]
    unnamed x10 -> x1, local copies, waits for them, and re-layouts: 13.4 us -> 1.77 us
    sub x1 -> x0, other arithmetic: 11.6 us -> none  [defects(): square = 2.0 - block[0] * block[0] - block[1] * block[1]]
    psum x1 -> x0, waiting for transfers between devices: 11.5 us -> none  [spread(): return lax.psum(jnp.where(mine, x, jnp.zeros_like(x)), axis)]
  transfers between devices with their start and end apart: 4 -> 0, of which waited for: 4 -> 0; matrix products, arithmetic and copies ran while one was open for 14% -> 0% of each run, Pallas kernels for 0% -> 0%
where the time goes in v2:
time: 91.6 us; the launch traced here: 91.4 us
  Pallas kernels  89 us (97%)
  local copies, waits for them, and re-layouts  1.77 us (2%)
    pallas_call x1, Pallas kernels, sums_of(): pl.pallas_call(kernel, out_shape=jax.ShapeDtypeStruct((rows, 2, COLS), F3...  89 us

profile of v2, /device:TPU:64, one launch (start us, length us, event | category | flops | bytes accessed | tf_op | source)
XLA Modules:
  0.0 91.4 jit_solution(14950631230853061947)
XLA Ops:
  0.7 89.0 %remainder_sums.1 = f32[96,2,512]{2,1,0:T(2,128)} custom-call(f32[2,256,6144]{2,1,0:T(8,128)} %m_ref.1, s32[1,256]{1,0:T(1,128)} %bitcast.4, f32[1,256]{1,0:T(1,128)} %bitcast.5, f32[1,12288]{1,0:T(1,128)} %bitcast.3, s32[1]{0:T(128)S(6)} %copy.7.occ_ref), custom_call_target="tpu_custom_call" | custom-call | tf_op jit(solution)/shard_map/remainder_sums/pallas_call | solution.py:367
  89.6 1.8 %copy.8 = f32[96,2,512]{2,1,0:T(2,128)} copy(f32[96,2,512]{2,1,0:T(2,128)} %remainder_sums.1) | data formatting | bytes 786432

commit v3 on v2

--- a/solution.py
+++ b/solution.py
@@ -15,10 +15,11 @@
 GA_BAND = ("ga", "band_0", "band_1", "band_2", "band_3")
 MESH = pl.DeviceIdType.MESH
 Z_ORDER = (2, 3, 1, 0)
+Z_GROUP = (0, 1, 1, 2)
 RING = 4
 PARTS = 2
 ROUNDS = 4 * PARTS
-LAGS = (1, 2, 3, 4, 5)
+LAGS = (2, 3, 4, 5)
 SLOTS = 4
 STAGES = 4
 F32 = jnp.float32
@@ -31,12 +32,12 @@
 
 
 def kernel(
-    m_ref, bi_ref, bw_ref, coul_ref, occ_ref, o_ref,
-    at, wst, rdef, cdef, coef, rowc, stage, slab, psend, pin,
+    m_ref, bi_in, bw_in, coul_in, occ_ref, o_ref,
+    bi_ref, bw_ref, coul_ref, at, wst, rdef, cdef, coef, rowc, stage, slab, psend, pin,
     q, t1in, din, r1, zin, rz, t1in2, din2,
     stage_sem, slab_copy, slab_send, slab_recv, pair_send, pair_recv,
     t1_send, t1_recv, in_send, in_recv, t1_send2, t1_recv2, in_send2, in_recv2,
-    z_send, z_recv,
+    z_send, z_recv, small_sem,
 ):
     rows = o_ref.shape[0]
     part = rows // PARTS
@@ -88,13 +89,33 @@
         for j in range(n_chunks):
             slab_local(j).start()
 
-    for i in range(STAGES):
+    small = [
+        pltpu.make_async_copy(src, dst, small_sem.at[n])
+        for n, (src, dst) in enumerate(((bi_in, bi_ref), (bw_in, bw_ref), (coul_in, coul_ref)))
+    ]
+    stage_copy(jnp.int32(0)).start()
+    for copy in small:
+        copy.start()
+    for i in range(1, STAGES):
         stage_copy(jnp.int32(i)).start()
+    for copy in small:
+        copy.wait()
 
     c_row = (0.5 - (bi_ref[...] < occ_ref[0]).astype(F32)) * bw_ref[...]
     for i in range(nb // LANES):
         piece = c_row[:, i * LANES : (i + 1) * LANES]
         coef[pl.ds(i * LANES, LANES), :] = jnp.broadcast_to(piece, (LANES, LANES)).T
+
+    @pl.when(ga == 0)
+    def _():
+        pltpu.make_async_copy(slab, slab, slab_copy.at[0]).wait()
+
+    pl.semaphore_wait(barrier, len(peers))
+
+    @pl.when(ga == 0)
+    def _():
+        for j in range(n_chunks):
+            slab_remote(j).start()
 
     total_g = coul_ref.shape[1]
     row_start = ga * ng + (((y * 2 + z) * RING + x) * 2 + core) * rows
@@ -133,20 +154,7 @@
 
         return carry
 
-    prep(jnp.int32(0), 0)
-
-    @pl.when(ga == 0)
-    def _():
-        pltpu.make_async_copy(slab, slab, slab_copy.at[0]).wait()
-
-    pl.semaphore_wait(barrier, len(peers))
-
-    @pl.when(ga == 0)
-    def _():
-        for j in range(n_chunks):
-            slab_remote(j).start()
-
-    lax.fori_loop(1, 2 * RING, prep, 0)
+    lax.fori_loop(0, RING + RING * ga, prep, 0)
 
     def weights(j):
         @pl.when(ga == 1)
@@ -193,6 +201,10 @@
             weights(r // PARTS)
 
         def one_pair(g, carry):
+            @pl.when((r == 0) & (g == 1))
+            def _():
+                lax.fori_loop(RING + RING * ga, 2 * RING, prep, 0)
+
             @pl.when(r >= 2)
             def _():
                 pair_copy(r - 2, g).wait_send()
@@ -279,12 +291,12 @@
         e = lax.rem(two.axes[k][1] + Z_ORDER[m], RING)
         return pltpu.make_async_remote_copy(
             r1.at[lax.rem(r, SLOTS), k, 1 - z, e], zin.at[r, k, e],
-            z_send.at[lax.rem(r, SLOTS), min(m, 1)], z_recv.at[r, min(m, 1)],
+            z_send.at[lax.rem(r, SLOTS), Z_GROUP[m]], z_recv.at[r, Z_GROUP[m]],
             device_id={"band_1": 1 - z}, device_id_type=MESH,
         )
 
     def z_whole(r, n):
-        ref = zin.at[r, :, pl.ds(n, 1 + 2 * n)]
+        ref = zin.at[r, :, pl.ds(n, Z_GROUP.count(n))]
         return size_of(ref, z_send.at[lax.rem(r, SLOTS), n], z_recv.at[r, n])
 
     def to_other_z(t):
@@ -297,10 +309,10 @@
 
     def from_other_z(t):
         slot = lax.rem(t, SLOTS)
-        for which, ms in ((0, (0,)), (1, (1, 2, 3))):
+        for which in range(2):
             z_whole(t, which).wait_recv()
             for k in range(2):
-                for m in ms:
+                for m in (m for m in range(RING) if Z_GROUP[m] == which):
                     e = lax.rem(two.axes[k][1] + Z_ORDER[m], RING)
                     rz[slot, k, e] = r1[slot, k, z, e] + zin[t, k, e]
                 two.begin(t, which, k)
@@ -308,43 +320,53 @@
 
     def second_combine(t):
         two.combine(t)
-        for n in range(2):
+        for n in range(3):
             z_whole(t, n).wait_send()
 
     def finish(t):
         down_to = pl.ds(pl.multiple_of(lax.rem(t, PARTS) * part, 8), part)
         lanes = pl.multiple_of((t // PARTS) * LANES, LANES)
         weight = jnp.sqrt(rowc[down_to, :] * coul_ref[:, pl.ds(lanes, LANES)]) * scale
+        z_whole(t, 2).wait_recv()
         two.arrived(t)
+        slot = lax.rem(t, SLOTS)
         for k in range(2):
+            me = two.axes[k][1]
+            rz[slot, k, me] = r1[slot, k, z, me] + zin[t, k, me]
             o_ref[down_to, k, pl.ds(lanes, LANES)] = two.total(t, k) * weight
         two.sent(t)
 
-    give(jnp.int32(0))
-
     def step(r, carry):
+        @pl.when((r >= 0) & (r < ROUNDS))
+        def _():
+            keep(r)
+            for k in range(2):
+                one.begin(r, 0, k)
+
+        @pl.when((r >= 1) & (r < ROUNDS + 1))
+        def _():
+            one.combine(r - 1)
+
+        @pl.when((r >= 0) & (r < ROUNDS))
+        def _():
+            for k in range(2):
+                one.begin(r, 1, k)
+
         @pl.when(r + 1 < ROUNDS)
         def _():
             give(r + 1)
-
-        @pl.when(r < ROUNDS)
-        def _():
-            keep(r)
-            for which in (0, 1):
-                for k in range(2):
-                    one.begin(r, which, k)
 
         def late(lag, stage_work):
             @pl.when((r >= lag) & (r < ROUNDS + lag))
             def _():
                 stage_work(r - lag)
 
-        for lag, stage_work in zip(LAGS, (one.combine, to_other_z, from_other_z, second_combine, finish)):
+        for lag, stage_work in zip(LAGS, (to_other_z, from_other_z, second_combine, finish)):
             late(lag, stage_work)
 
         return carry
 
-    lax.fori_loop(0, ROUNDS + LAGS[-1], step, 0)
+    lax.fori_loop(-1, ROUNDS + LAGS[-1], step, 0)
 
     for g in range(2):
         pair_copy(ROUNDS - 2, g).wait_send()
@@ -367,9 +389,12 @@
     return pl.pallas_call(
         kernel,
         out_shape=jax.ShapeDtypeStruct((rows, 2, COLS), F32),
-        in_specs=[pl.BlockSpec(memory_space=pl.ANY), vmem, vmem, vmem, pl.BlockSpec(memory_space=pltpu.SMEM)],
+        in_specs=[pl.BlockSpec(memory_space=pl.ANY)] * 4 + [pl.BlockSpec(memory_space=pltpu.SMEM)],
         out_specs=vmem,
         scratch_shapes=[
+            pltpu.VMEM((1, nb), jnp.int32),
+            pltpu.VMEM((1, nb), F32),
+            pltpu.VMEM((1, coulomb.shape[0]), F32),
             pltpu.VMEM((ng, 4 * nb), BF16),
             pltpu.VMEM((2, 6 * nb, 2 * LANES), BF16),
             pltpu.VMEM((ng, LANES), F32),
@@ -391,7 +416,7 @@
             dma((STAGES,)), dma((1,)), dma((1,)), dma((n_chunks,)),
             dma((2, 2)), dma((ROUNDS, 2)),
             *ring(), *ring(),
-            dma((SLOTS, 2)), dma((ROUNDS, 2)),
+            dma((SLOTS, 3)), dma((ROUNDS, 3)), dma((3,)),
         ],
         compiler_params=pltpu.CompilerParams(
             collective_id=0, has_side_effects=True, vmem_limit_bytes=67043328

time: 91.6 us -> 89.9 us (0.981)
  Pallas kernels: 89 us -> 87 us
    pallas_call x1, Pallas kernels: 89 us -> 87 us  [sums_of(): pl.pallas_call(kernel, out_shape=jax.ShapeDtypeStruct((rows, 2, COLS), F3...]
where the time goes in v3:
time: 89.9 us; the launch traced here: 89.4 us
  Pallas kernels  87 us (97%)
  local copies, waits for them, and re-layouts  1.77 us (2%)
    pallas_call x1, Pallas kernels, sums_of(): pl.pallas_call(kernel, out_shape=jax.ShapeDtypeStruct((rows, 2, COLS), F3...  87 us

profile of v3, /device:TPU:64, one launch (start us, length us, event | category | flops | bytes accessed | tf_op | source)
XLA Modules:
  0.0 89.4 jit_solution(10623263946911532769)
XLA Ops:
  0.7 87.0 %remainder_sums.1 = f32[96,2,512]{2,1,0:T(2,128)} custom-call(f32[2,256,6144]{2,1,0:T(8,128)} %m_ref.1, s32[1,256]{1,0:T(1,128)} %bitcast.4, f32[1,256]{1,0:T(1,128)} %bitcast.5, f32[1,12288]{1,0:T(1,128)} %bitcast.3, s32[1]{0:T(128)S(6)} %copy.7.occ_ref), custom_call_target="tpu_custom_call" | custom-call | tf_op jit(solution)/shard_map/remainder_sums/pallas_call | solution.py:389
  87.6 1.8 %copy.8 = f32[96,2,512]{2,1,0:T(2,128)} copy(f32[96,2,512]{2,1,0:T(2,128)} %remainder_sums.1) | data formatting | bytes 786432

commit v4 on v3

--- a/solution.py
+++ b/solution.py
@@ -40,6 +40,7 @@
     z_send, z_recv, small_sem,
 ):
     rows = o_ref.shape[0]
+    half = rows // 2
     part = rows // PARTS
     nb = m_ref.shape[1]
     ng = m_ref.shape[2]
@@ -146,7 +147,7 @@
             rdef[here, :] = jnp.broadcast_to(share, (LANES, LANES)).T
             return carry
 
-        lax.fori_loop(0, group // LANES, column, 0)
+        lax.fori_loop(0, group // LANES, column, 0, unroll=2)
 
         @pl.when(i + STAGES < 2 * RING)
         def _():
@@ -154,7 +155,7 @@
 
         return carry
 
-    lax.fori_loop(0, RING + RING * ga, prep, 0)
+    lax.fori_loop(0, 2 + (2 * RING - 2) * ga, prep, 0)
 
     def weights(j):
         @pl.when(ga == 1)
@@ -174,14 +175,14 @@
             wst[w, at_row + nb : at_row + 2 * nb, 0:LANES] = bb
             wst[w, at_row + nb : at_row + 2 * nb, LANES:] = -aa
 
-    pieces = [(y2, zd, xx) for y2 in range(2) for zd in range(2) for xx in range(RING)]
+    pieces = [(zd, xx) for zd in range(2) for xx in range(RING)]
 
     def product(r, g, parity):
         w = lax.rem(r // PARTS, 2)
-        base = g * (4 * group) + parity * rows + lax.rem(r, PARTS) * part
+        base = g * (2 * group) + parity * rows + lax.rem(r, PARTS) * part
         spots = [
-            pl.ds(pl.multiple_of(base + (2 * y2 + zd) * group + 2 * xx * rows, 16), part)
-            for y2, zd, xx in pieces
+            pl.ds(pl.multiple_of(base + zd * group + 2 * xx * rows, 16), part)
+            for zd, xx in pieces
         ]
         left = jnp.concatenate([at[s, :] for s in spots], 0)
         left = jnp.concatenate([left, left[:, : 2 * nb]], 1)
@@ -201,22 +202,23 @@
             weights(r // PARTS)
 
         def one_pair(g, carry):
-            @pl.when((r == 0) & (g == 1))
+            @pl.when((r == 0) & (g > 0))
             def _():
-                lax.fori_loop(RING + RING * ga, 2 * RING, prep, 0)
+                first = 2 * g * (1 - ga)
+                lax.fori_loop(first, first + 2 * (1 - ga), prep, 0)
 
             @pl.when(r >= 2)
             def _():
                 pair_copy(r - 2, g).wait_send()
 
             re, im = product(r, g, 1 - core)
-            for n, (y2, zd, xx) in enumerate(pieces):
-                psend[lax.rem(r, 2), g, 0, zd, y2, xx] = re[n * part : (n + 1) * part]
-                psend[lax.rem(r, 2), g, 1, zd, y2, xx] = im[n * part : (n + 1) * part]
+            for n, (zd, xx) in enumerate(pieces):
+                psend[lax.rem(r, 2), g, 0, zd, xx] = re[n * part : (n + 1) * part]
+                psend[lax.rem(r, 2), g, 1, zd, xx] = im[n * part : (n + 1) * part]
             pair_copy(r, g).start()
             return carry
 
-        lax.fori_loop(0, 2, one_pair, 0)
+        lax.fori_loop(0, RING, one_pair, 0)
 
     def keep(r):
         slot = lax.rem(r, SLOTS)
@@ -224,34 +226,34 @@
         def one_pair(g, carry):
             re, im = product(r, g, core)
             pair_copy(r, g).wait_recv()
-            for n, (y2, zd, xx) in enumerate(pieces):
-                q[slot, 0, xx, zd, 2 * g + y2] = re[n * part : (n + 1) * part] + pin[r, g, 0, zd, y2, xx]
-                q[slot, 1, 2 * g + y2, zd, xx] = im[n * part : (n + 1) * part] + pin[r, g, 1, zd, y2, xx]
+            for n, (zd, xx) in enumerate(pieces):
+                q[slot, 0, xx, zd, g] = re[n * part : (n + 1) * part] + pin[r, g, 0, zd, xx]
+                q[slot, 1, g, zd, xx] = im[n * part : (n + 1) * part] + pin[r, g, 1, zd, xx]
             return carry
 
-        lax.fori_loop(0, 2, one_pair, 0)
+        lax.fori_loop(0, RING, one_pair, 0)
 
     class Stage:
-        def __init__(self, held, tin, landed, cut, sems, axes):
-            self.held, self.tin, self.landed = held, tin, landed
+        def __init__(self, held, slots, tin, landed, cut, sems, axes):
+            self.held, self.slots, self.tin, self.landed = held, slots, tin, landed
             self.cut, self.sems, self.axes = cut, sems, axes
 
         def send(self, which, r, k, way):
             name, me = self.axes[k]
             to = up(me) if way == 0 else down(me)
             here = self.cut(way if which != 1 else 1 - way)
-            chunk = (lax.rem(r, SLOTS), k, opposite(me) if which == 0 else to)
+            chunk = (lax.rem(r, self.slots), k, opposite(me) if which == 0 else to)
             src = self.held.at[chunk + here]
             dst = self.tin.at[r, k, way] if which == 0 else self.landed.at[(r, k, way) + here]
             ss, rs = self.sems[min(which, 1)]
             return pltpu.make_async_remote_copy(
-                src, dst, ss.at[lax.rem(r, SLOTS)], rs.at[r], device_id={name: to}, device_id_type=MESH
+                src, dst, ss.at[lax.rem(r, self.slots)], rs.at[r], device_id={name: to}, device_id_type=MESH
             )
 
         def whole(self, which, r):
             ref = (self.tin if which == 0 else self.landed).at[r]
             ss, rs = self.sems[which]
-            return size_of(ref, ss.at[lax.rem(r, SLOTS)], rs.at[r])
+            return size_of(ref, ss.at[lax.rem(r, self.slots)], rs.at[r])
 
         def begin(self, r, which, k):
             for way in range(2):
@@ -263,7 +265,7 @@
                 me = self.axes[k][1]
                 for way in range(2):
                     to = up(me) if way == 0 else down(me)
-                    here = (lax.rem(r, SLOTS), k, to) + self.cut(way)
+                    here = (lax.rem(r, self.slots), k, to) + self.cut(way)
                     self.held[here] += self.tin[r, k, way]
                     self.send(2, r, k, way).start()
 
@@ -271,7 +273,7 @@
             self.whole(1, r).wait_recv()
 
         def total(self, r, k):
-            return self.held[lax.rem(r, SLOTS), k, self.axes[k][1]] + self.landed[r, k, 0] + self.landed[r, k, 1]
+            return self.held[lax.rem(r, self.slots), k, self.axes[k][1]] + self.landed[r, k, 0] + self.landed[r, k, 1]
 
         def sent(self, r):
             self.whole(0, r).wait_send()
@@ -279,11 +281,11 @@
 
     along_x, along_y = ("band_2", x), ("band_0", y)
     one = Stage(
-        q, t1in, din, lambda h: (h,),
+        q, SLOTS, t1in, din, lambda h: (h,),
         ((t1_send, t1_recv), (in_send, in_recv)), (along_x, along_y),
     )
     two = Stage(
-        rz, t1in2, din2, lambda h: (pl.ds(h * (part // 2), part // 2),),
+        rz, 2, t1in2, din2, lambda h: (pl.ds(h * half, half),),
         ((t1_send2, t1_recv2), (in_send2, in_recv2)), (along_y, along_x),
     )
 
@@ -307,34 +309,57 @@
             for k in range(2):
                 z_copy(t, k, m).start()
 
+    def sub_rows(t):
+        return pl.ds(pl.multiple_of(lax.rem(t, PARTS) * part, 8), part)
+
+    def join(t, k, m):
+        e = lax.rem(two.axes[k][1] + Z_ORDER[m], RING)
+        here = (lax.rem(t // PARTS, 2), k, e, sub_rows(t), slice(None))
+        rz[here] = r1[lax.rem(t, SLOTS), k, z, e] + zin[t, k, e]
+
     def from_other_z(t):
-        slot = lax.rem(t, SLOTS)
+        last = lax.rem(t, PARTS) == PARTS - 1
         for which in range(2):
             z_whole(t, which).wait_recv()
             for k in range(2):
                 for m in (m for m in range(RING) if Z_GROUP[m] == which):
-                    e = lax.rem(two.axes[k][1] + Z_ORDER[m], RING)
-                    rz[slot, k, e] = r1[slot, k, z, e] + zin[t, k, e]
-                two.begin(t, which, k)
+                    join(t, k, m)
+
+            @pl.when(last)
+            def _():
+                for k in range(2):
+                    two.begin(t // PARTS, which, k)
+
+        z_whole_last(t, lax.rem(t, PARTS) < PARTS - 1)
         one.sent(t)
 
+    def z_whole_last(t, now):
+        @pl.when(now)
+        def _():
+            z_whole(t, 2).wait_recv()
+            for k in range(2):
+                join(t, k, RING - 1)
+
     def second_combine(t):
-        two.combine(t)
+        @pl.when(lax.rem(t, PARTS) == PARTS - 1)
+        def _():
+            two.combine(t // PARTS)
+
         for n in range(3):
             z_whole(t, n).wait_send()
 
     def finish(t):
-        down_to = pl.ds(pl.multiple_of(lax.rem(t, PARTS) * part, 8), part)
-        lanes = pl.multiple_of((t // PARTS) * LANES, LANES)
-        weight = jnp.sqrt(rowc[down_to, :] * coul_ref[:, pl.ds(lanes, LANES)]) * scale
-        z_whole(t, 2).wait_recv()
-        two.arrived(t)
-        slot = lax.rem(t, SLOTS)
-        for k in range(2):
-            me = two.axes[k][1]
-            rz[slot, k, me] = r1[slot, k, z, me] + zin[t, k, me]
-            o_ref[down_to, k, pl.ds(lanes, LANES)] = two.total(t, k) * weight
-        two.sent(t)
+        z_whole_last(t, lax.rem(t, PARTS) == PARTS - 1)
+
+        @pl.when(lax.rem(t, PARTS) == PARTS - 1)
+        def _():
+            j = t // PARTS
+            lanes = pl.ds(pl.multiple_of(j * LANES, LANES), LANES)
+            weight = jnp.sqrt(rowc[0:rows, :] * coul_ref[:, lanes]) * scale
+            two.arrived(j)
+            for k in range(2):
+                o_ref[:, k, lanes] = two.total(j, k) * weight
+            two.sent(j)
 
     def step(r, carry):
         @pl.when((r >= 0) & (r < ROUNDS))
@@ -368,7 +393,7 @@
 
     lax.fori_loop(-1, ROUNDS + LAGS[-1], step, 0)
 
-    for g in range(2):
+    for g in range(RING):
         pair_copy(ROUNDS - 2, g).wait_send()
         pair_copy(ROUNDS - 1, g).wait_send()
 
@@ -384,7 +409,7 @@
     group = 2 * RING * rows
     n_chunks = COLS // LANES
     dma = pltpu.SemaphoreType.DMA
-    ring = lambda: [dma((n,)) for n in (SLOTS, ROUNDS, SLOTS, ROUNDS)]
+    ring = lambda slots, n: [dma((slots,)), dma((n,)), dma((slots,)), dma((n,))]
     vmem = pl.BlockSpec(memory_space=pltpu.VMEM)
     return pl.pallas_call(
         kernel,
@@ -403,19 +428,19 @@
             pltpu.VMEM((LANES, LANES), F32),
             pltpu.VMEM((STAGES, 2, nb, group), F32),
             pltpu.VMEM((n_chunks, 2, nb, LANES), F32),
-            pltpu.VMEM((2, 2, 2, 2, 2, RING, part, LANES), F32),
-            pltpu.VMEM((ROUNDS, 2, 2, 2, 2, RING, part, LANES), F32),
+            pltpu.VMEM((2, RING, 2, 2, RING, part, LANES), F32),
+            pltpu.VMEM((ROUNDS, RING, 2, 2, RING, part, LANES), F32),
             pltpu.VMEM((SLOTS, 2, RING, 2, RING, part, LANES), F32),
             pltpu.VMEM((ROUNDS, 2, 2, RING, part, LANES), F32),
             pltpu.VMEM((ROUNDS, 2, 2, 2, RING, part, LANES), F32),
             pltpu.VMEM((SLOTS, 2, 2, RING, part, LANES), F32),
             pltpu.VMEM((ROUNDS, 2, RING, part, LANES), F32),
-            pltpu.VMEM((SLOTS, 2, RING, part, LANES), F32),
-            pltpu.VMEM((ROUNDS, 2, 2, part // 2, LANES), F32),
-            pltpu.VMEM((ROUNDS, 2, 2, part, LANES), F32),
+            pltpu.VMEM((2, 2, RING, rows, LANES), F32),
+            pltpu.VMEM((n_chunks, 2, 2, rows // 2, LANES), F32),
+            pltpu.VMEM((n_chunks, 2, 2, rows, LANES), F32),
             dma((STAGES,)), dma((1,)), dma((1,)), dma((n_chunks,)),
-            dma((2, 2)), dma((ROUNDS, 2)),
-            *ring(), *ring(),
+            dma((2, RING)), dma((ROUNDS, RING)),
+            *ring(SLOTS, ROUNDS), *ring(2, n_chunks),
             dma((SLOTS, 3)), dma((ROUNDS, 3)), dma((3,)),
         ],
         compiler_params=pltpu.CompilerParams(

time: 89.9 us -> 88.9 us (0.989)
  no operation moved by 1% of the time
where the time goes in v4:
time: 88.9 us; the launch traced here: 88.8 us
  Pallas kernels  86.3 us (97%)
  local copies, waits for them, and re-layouts  1.77 us (2%)
    pallas_call x1, Pallas kernels, sums_of(): pl.pallas_call(kernel, out_shape=jax.ShapeDtypeStruct((rows, 2, COLS), F3...  86.3 us

profile of v4, /device:TPU:64, one launch (start us, length us, event | category | flops | bytes accessed | tf_op | source)
XLA Modules:
  0.0 88.8 jit_solution(8203358792276352739)
XLA Ops:
  0.7 86.3 %remainder_sums.1 = f32[96,2,512]{2,1,0:T(2,128)} custom-call(f32[2,256,6144]{2,1,0:T(8,128)} %m_ref.1, s32[1,256]{1,0:T(1,128)} %bitcast.4, f32[1,256]{1,0:T(1,128)} %bitcast.5, f32[1,12288]{1,0:T(1,128)} %bitcast.3, s32[1]{0:T(128)S(6)} %copy.7.occ_ref), custom_call_target="tpu_custom_call" | custom-call | tf_op jit(solution)/shard_map/remainder_sums/pallas_call | solution.py:414
  87.0 1.8 %copy.8 = f32[96,2,512]{2,1,0:T(2,128)} copy(f32[96,2,512]{2,1,0:T(2,128)} %remainder_sums.1) | data formatting | bytes 786432

commit v5 on v4

--- a/solution.py
+++ b/solution.py
@@ -77,7 +77,7 @@
         )
 
     def slab_local(j):
-        return pltpu.make_async_copy(m_ref.at[:, :, pl.ds(j * LANES, LANES)], slab.at[j], slab_copy.at[0])
+        return pltpu.make_async_copy(m_ref.at[:, :, pl.ds(j * LANES, LANES)], slab.at[j], slab_copy.at[min(j, 1)])
 
     def slab_remote(j):
         return pltpu.make_async_remote_copy(
@@ -87,8 +87,7 @@
 
     @pl.when(ga == 0)
     def _():
-        for j in range(n_chunks):
-            slab_local(j).start()
+        slab_local(0).start()
 
     small = [
         pltpu.make_async_copy(src, dst, small_sem.at[n])
@@ -99,6 +98,25 @@
         copy.start()
     for i in range(1, STAGES):
         stage_copy(jnp.int32(i)).start()
+    @pl.when(ga == 0)
+    def _():
+        for j in range(1, n_chunks):
+            slab_local(j).start()
+
+    @pl.when(ga == 0)
+    def _():
+        slab_local(0).wait()
+
+    pl.semaphore_wait(barrier, len(peers))
+
+    @pl.when(ga == 0)
+    def _():
+        slab_remote(0).start()
+        rest = slab.at[pl.ds(1, n_chunks - 1)]
+        pltpu.make_async_copy(rest, rest, slab_copy.at[1]).wait()
+        for j in range(1, n_chunks):
+            slab_remote(j).start()
+
     for copy in small:
         copy.wait()
 
@@ -106,17 +124,6 @@
     for i in range(nb // LANES):
         piece = c_row[:, i * LANES : (i + 1) * LANES]
         coef[pl.ds(i * LANES, LANES), :] = jnp.broadcast_to(piece, (LANES, LANES)).T
-
-    @pl.when(ga == 0)
-    def _():
-        pltpu.make_async_copy(slab, slab, slab_copy.at[0]).wait()
-
-    pl.semaphore_wait(barrier, len(peers))
-
-    @pl.when(ga == 0)
-    def _():
-        for j in range(n_chunks):
-            slab_remote(j).start()
 
     total_g = coul_ref.shape[1]
     row_start = ga * ng + (((y * 2 + z) * RING + x) * 2 + core) * rows
@@ -192,7 +199,7 @@
 
     def pair_copy(r, g):
         return pltpu.make_async_remote_copy(
-            psend.at[lax.rem(r, 2), g], pin.at[r, g], pair_send.at[lax.rem(r, 2), g], pair_recv.at[r, g],
+            psend.at[lax.rem(r, 2), g], pin.at[lax.rem(r, 2), g], pair_send.at[lax.rem(r, 2), g], pair_recv.at[lax.rem(r, 2), g],
             device_id={"band_3": 1 - core}, device_id_type=MESH,
         )
 
@@ -227,8 +234,8 @@
             re, im = product(r, g, core)
             pair_copy(r, g).wait_recv()
             for n, (zd, xx) in enumerate(pieces):
-                q[slot, 0, xx, zd, g] = re[n * part : (n + 1) * part] + pin[r, g, 0, zd, xx]
-                q[slot, 1, g, zd, xx] = im[n * part : (n + 1) * part] + pin[r, g, 1, zd, xx]
+                q[slot, 0, xx, zd, g] = re[n * part : (n + 1) * part] + pin[lax.rem(r, 2), g, 0, zd, xx]
+                q[slot, 1, g, zd, xx] = im[n * part : (n + 1) * part] + pin[lax.rem(r, 2), g, 1, zd, xx]
             return carry
 
         lax.fori_loop(0, RING, one_pair, 0)
@@ -368,6 +375,10 @@
             for k in range(2):
                 one.begin(r, 0, k)
 
+        @pl.when(r + 1 < ROUNDS)
+        def _():
+            give(r + 1)
+
         @pl.when((r >= 1) & (r < ROUNDS + 1))
         def _():
             one.combine(r - 1)
@@ -376,10 +387,6 @@
         def _():
             for k in range(2):
                 one.begin(r, 1, k)
-
-        @pl.when(r + 1 < ROUNDS)
-        def _():
-            give(r + 1)
 
         def late(lag, stage_work):
             @pl.when((r >= lag) & (r < ROUNDS + lag))
@@ -429,7 +436,7 @@
             pltpu.VMEM((STAGES, 2, nb, group), F32),
             pltpu.VMEM((n_chunks, 2, nb, LANES), F32),
             pltpu.VMEM((2, RING, 2, 2, RING, part, LANES), F32),
-            pltpu.VMEM((ROUNDS, RING, 2, 2, RING, part, LANES), F32),
+            pltpu.VMEM((2, RING, 2, 2, RING, part, LANES), F32),
             pltpu.VMEM((SLOTS, 2, RING, 2, RING, part, LANES), F32),
             pltpu.VMEM((ROUNDS, 2, 2, RING, part, LANES), F32),
             pltpu.VMEM((ROUNDS, 2, 2, 2, RING, part, LANES), F32),
@@ -438,13 +445,13 @@
             pltpu.VMEM((2, 2, RING, rows, LANES), F32),
             pltpu.VMEM((n_chunks, 2, 2, rows // 2, LANES), F32),
             pltpu.VMEM((n_chunks, 2, 2, rows, LANES), F32),
-            dma((STAGES,)), dma((1,)), dma((1,)), dma((n_chunks,)),
-            dma((2, RING)), dma((ROUNDS, RING)),
+            dma((STAGES,)), dma((2,)), dma((1,)), dma((n_chunks,)),
+            dma((2, RING)), dma((2, RING)),
             *ring(SLOTS, ROUNDS), *ring(2, n_chunks),
             dma((SLOTS, 3)), dma((ROUNDS, 3)), dma((3,)),
         ],
         compiler_params=pltpu.CompilerParams(
-            collective_id=0, has_side_effects=True, vmem_limit_bytes=67043328
+            collective_id=0, has_side_effects=True, vmem_limit_bytes=54*1024*1024
         ),
         name="remainder_sums",
     )(

time: 88.9 us -> 88.4 us (level)
  no operation moved by 1% of the time
where the time goes in v5:
time: 88.4 us; the launch traced here: 88.2 us
  Pallas kernels  85.8 us (97%)
  local copies, waits for them, and re-layouts  1.77 us (2%)
    pallas_call x1, Pallas kernels, sums_of(): pl.pallas_call(kernel, out_shape=jax.ShapeDtypeStruct((rows, 2, COLS), F3...  85.8 us

profile of v5, /device:TPU:64, one launch (start us, length us, event | category | flops | bytes accessed | tf_op | source)
XLA Modules:
  0.0 88.2 jit_solution(3547301079718020676)
XLA Ops:
  0.7 85.8 %remainder_sums.1 = f32[96,2,512]{2,1,0:T(2,128)} custom-call(f32[2,256,6144]{2,1,0:T(8,128)} %m_ref.1, s32[1,256]{1,0:T(1,128)} %bitcast.4, f32[1,256]{1,0:T(1,128)} %bitcast.5, f32[1,12288]{1,0:T(1,128)} %bitcast.3, s32[1]{0:T(128)S(6)} %copy.7.occ_ref), custom_call_target="tpu_custom_call" | custom-call | tf_op jit(solution)/shard_map/remainder_sums/pallas_call | solution.py:421
  86.5 1.8 %copy.8 = f32[96,2,512]{2,1,0:T(2,128)} copy(f32[96,2,512]{2,1,0:T(2,128)} %remainder_sums.1) | data formatting | bytes 786432
